TPU v7x, 128 devices: a whole 4x4x4 slice. The times are simulated.
128 devices in a mesh: dp: 8 (over x, z_lo), rep: 16 (over z_hi, y, core).
Axes of the slice: x: 4, y: 4, z: 4 (z_hi: 2, z_lo: 2; z = z_hi * 2 + z_lo), core: 2. Of those that a mesh axis runs over, the one named last changes fastest.
Arguments:
- queries: bfloat16 [65536, 2048], P(('dp', 'rep')), may hold values from -32 to 32
- key_rows: bfloat16 [65536, 2048], P(('dp', 'rep')), may hold values from -32 to 32
- values: bfloat16 [65536, 2048], P(('dp', 'rep')), may hold values from -6 to 6
- upstream: bfloat16 [65536, 2048], P(('dp', 'rep')), may hold values from -24 to 24
- out_weight: bfloat16 [2048, 2048], P(('dp', 'rep')), may hold values from -0.125 to 0.125
- sample_ids: int32 [128, 512], P(('dp', 'rep')), may hold values from 0 to 3, as said below
Outputs:
- grad_queries: bfloat16 [65536, 2048], P(('dp', 'rep'))
- grad_keys: bfloat16 [65536, 2048], P(('dp', 'rep'))
- grad_values: bfloat16 [65536, 2048], P(('dp', 'rep'))
- grad_weight: float32 [2048, 2048], P(('dp', 'rep'))
Inputs may be any that keep to these rules, and one draw needn't show every extreme that they name: `sample_ids`: within a row the ids never fall, every row starts with 0 and ends with 3, and the tokens of one sample are contiguous.
All inputs are finite; a program needn't handle non-finite values.
Results may differ from a plain program's by a relative error of at most 0.015.
Values may be sent and summed in bfloat16 or wider, within the bound.
A program may use at most 192 MiB of HBM per device.

v0:
```python
import math

import jax
import jax.numpy as jnp
from jax import lax
from jax.sharding import Mesh
from jax.sharding import PartitionSpec as P

H = 16
DH = 128
DP = ("dp_0", "dp_1")
DP_REP = ("dp_0", "dp_1", "rep")


def own_rows(terms, axes):
    running = terms.astype(jnp.bfloat16)
    for axis in axes:
        running = lax.psum_scatter(running, axis, scatter_dimension=0, tiled=True)
    return running.astype(jnp.float32)


def cut_along(value, dim, devices):
    before, after = (value.shape[:dim], value.shape[dim + 1 :])
    return jnp.moveaxis(value.reshape(*before, devices, -1, *after), dim, 0)


def sum_at_owner(value, axis, dim):
    devices = lax.axis_size(axis)
    pieces = lax.all_to_all(cut_along(value, dim, devices), axis, 0, 0, tiled=True)
    return jnp.sum(pieces.astype(jnp.float32), axis=0)


def sent_to_all(value, axis):
    devices = lax.axis_size(axis)
    return lax.all_to_all(
        jnp.broadcast_to(value[None], (devices, *value.shape)), axis, 0, 0, tiled=True
    )


def laid_out(pieces, dim):
    pieces = jnp.moveaxis(pieces, 0, dim)
    shape = pieces.shape
    return pieces.reshape(*shape[:dim], shape[dim] * shape[dim + 1], *shape[dim + 2 :])


def gathered_copies(value, axis, dim):
    pieces = sent_to_all(value, axis)
    return laid_out(pieces, dim)


def allowed_pairs(ids_row):
    positions = jnp.arange(ids_row.shape[0], dtype=jnp.int32)
    causal = positions[None, :] <= positions[:, None]
    return jnp.logical_and(causal, ids_row[None, :] == ids_row[:, None])[None]


def attend_forward(query_block, key_block, value_block, ids_row):
    scaling = 1.0 / math.sqrt(DH)
    scores = (
        jnp.einsum("qhd,khd->hqk", query_block, key_block, preferred_element_type=jnp.float32)
        * scaling
    )
    allowed = allowed_pairs(ids_row)
    masked = jnp.where(allowed, scores, -jnp.inf)
    row_max = jnp.max(masked, axis=2, keepdims=True)
    raised = jnp.where(allowed, jnp.exp(masked - row_max), 0.0)
    probabilities = raised / jnp.sum(raised, axis=2, keepdims=True)
    probs_low = probabilities.astype(jnp.bfloat16)
    attended = jnp.einsum(
        "hqk,khd->qhd", probs_low, value_block, preferred_element_type=jnp.float32
    ).astype(jnp.bfloat16)
    return (probabilities, probs_low, attended)


def attend_backward(probabilities, probs_low, query_block, key_block, value_block, grad_block):
    scaling = 1.0 / math.sqrt(DH)
    grad_values = jnp.einsum(
        "hqk,qhd->khd", probs_low, grad_block, preferred_element_type=jnp.float32
    ).astype(jnp.bfloat16)
    grad_probs = jnp.einsum(
        "qhd,khd->hqk", grad_block, value_block, preferred_element_type=jnp.float32
    )
    row_inner = jnp.sum(probabilities * grad_probs, axis=2, keepdims=True)
    grad_scores = (probabilities * (grad_probs - row_inner)).astype(jnp.bfloat16)
    grad_queries = (
        scaling
        * jnp.einsum("hqk,khd->qhd", grad_scores, key_block, preferred_element_type=jnp.float32)
    ).astype(jnp.bfloat16)
    grad_keys = (
        scaling
        * jnp.einsum("hqk,qhd->khd", grad_scores, query_block, preferred_element_type=jnp.float32)
    ).astype(jnp.bfloat16)
    return (grad_queries, grad_keys, grad_values)


def shards(queries, key_rows, values, upstream, out_weight, sample_ids):
    seq_count = sample_ids.shape[0]
    seq_len = sample_ids.shape[1]
    tok_rows = queries.shape[0]
    hidden_width = queries.shape[1]
    total_tokens = tok_rows * lax.axis_size(DP) * lax.axis_size("rep")
    split_shape = (seq_count, seq_len, H, DH)
    query_seqs = queries.reshape(split_shape)
    key_seqs = key_rows.reshape(split_shape)
    value_seqs = values.reshape(split_shape)
    seq_index = 0
    probabilities, probs_low, attended = attend_forward(
        query_seqs[seq_index], key_seqs[seq_index], value_seqs[seq_index], sample_ids[seq_index]
    )
    kept_probs = [(probabilities, probs_low)]
    attended_parts = attended.reshape(seq_len, hidden_width)
    columns = upstream
    group_sums = own_rows(
        lax.dot_general(
            columns, attended_parts, (((0,), (0,)), ((), ())), preferred_element_type=jnp.float32
        ),
        DP,
    )
    summed = sum_at_owner(group_sums.astype(jnp.bfloat16), "rep", 0)
    grad_weight = summed * (1.0 / math.sqrt(total_tokens))
    group_rows = gathered_copies(out_weight, "rep", 0)
    columns = upstream
    attended_sums = jnp.dot(
        columns,
        lax.all_gather(group_rows, DP, axis=0, tiled=True),
        preferred_element_type=jnp.float32,
    )
    grad_attended = attended_sums.astype(jnp.bfloat16).reshape(split_shape)
    seq_index = 0
    probabilities, probs_low = kept_probs[seq_index]
    grad_queries, grad_keys, grad_values = attend_backward(
        probabilities,
        probs_low,
        query_seqs[seq_index],
        key_seqs[seq_index],
        value_seqs[seq_index],
        grad_attended[seq_index],
    )
    query_parts = grad_queries.reshape(seq_len, hidden_width)
    key_parts = grad_keys.reshape(seq_len, hidden_width)
    value_parts = grad_values.reshape(seq_len, hidden_width)
    return (query_parts, key_parts, value_parts, grad_weight)


def solution(mesh):
    split = Mesh(mesh.devices.reshape(4, 2, mesh.shape["rep"]), ("dp_0", "dp_1", "rep"))
    return jax.shard_map(
        shards,
        mesh=split,
        in_specs=(
            P(DP_REP, None),
            P(DP_REP, None),
            P(DP_REP, None),
            P(DP_REP, None),
            P(DP_REP, None),
            P(DP_REP, None),
        ),
        out_specs=(P(DP_REP, None), P(DP_REP, None), P(DP_REP, None), P(DP_REP, None)),
        check_vma=False,
    )
```

profile of v0, /device:TPU:1, one launch (start us, length us, event | category | flops | bytes accessed | tf_op | source)
XLA Modules:
  0.0 309.7 jit_solution(14485813458067899327)
XLA Ops:
  8.0 0.0 copy-start
  8.0 0.0 all-gather.2.cloned.1.call-start
  8.1 1.1 broadcast_in_dim.33
  9.2 25.8 %all_to_all.10 = bf16[16,16,2048]{2,1,0:T(8,128)(2,1)} all-to-all(bf16[16,16,2048]{2,1,0:T(8,128)(2,1)S(1)} %broadcast_in_dim.33), channel_id=1, replica_groups=mesh['dp_0'=4,'dp_1'=2,'rep'=16] {'rep'}, dimensions={0} | all-to-all | bytes 2097152 | tf_op jit(solution)/shard_map/all_to_all | solution.py:35
  35.0 0.0 all-gather.2.cloned.1.call-update
  35.0 0.0 reduce-scatter.3.cloned.1.call-start
  35.0 3.9 %copy.46 = bf16[512,2048]{0,1:T(8,128)(2,1)} copy(bf16[512,2048]{1,0:T(8,128)(2,1)} %param.6) | data formatting | bytes 4194304 | tf_op jit(solution)/shard_map/squeeze;reshape | solution.py:108
  39.0 4.0 %copy.45 = bf16[512,2048]{0,1:T(8,128)(2,1)} copy(bf16[512,2048]{1,0:T(8,128)(2,1)} %param.7) | data formatting | bytes 4194304 | tf_op jit(solution)/shard_map/squeeze;reshape | solution.py:135
  42.9 3.9 %copy.48 = bf16[512,2048]{0,1:T(8,128)(2,1)} copy(bf16[512,2048]{1,0:T(8,128)(2,1)} %param.8) | data formatting | bytes 4194304 | tf_op jit(solution)/shard_map/squeeze;reshape | solution.py:136
  46.8 0.2 fusion.17
  47.1 12.0 %fusion.20 = (f32[16,512]{1,0:T(8,128)S(1)}, f32[16,512,512]{1,2,0:T(8,128)}) fusion(pred[512,512]{0,1:T(8,128)(4,1)S(1)} %fusion.17, bf16[512,16,128]{0,2,1:T(8,128)(2,1)} %bitcast.42, bf16[512,16,128]{0,2,1:T(8,128)(2,1)} %bitcast.37), kind=kOutput, calls=%fused_computation.27 | convolution fusion | flops 1094713856 | bytes 21266432 | tf_op jit(solution)/shard_map/sub | solution.py:66
  59.0 7.8 %fusion.12 = bf16[16,512,128]{1,2,0:T(8,128)(2,1)S(1)} fusion(bf16[512,16,128]{0,2,1:T(8,128)(2,1)} %bitcast.44, f32[16,512,512]{1,2,0:T(8,128)} %get-tuple-element.13, f32[16,512]{1,0:T(8,128)S(1)} %get-tuple-element.12), kind=kOutput, calls=%fused_computation.20 | convolution fusion | flops 1083179008 | bytes 21004288 | tf_op jit(solution)/shard_map/hqk,khd->qhd/dot_general | solution.py:69
  66.8 6.8 %convert_bitcast_fusion = bf16[2048,2048]{0,1:T(8,128)(2,1)} fusion(bf16[512,2048]{0,1:T(8,128)(2,1)S(1)} %bitcast.51, bf16[512,2048]{1,0:T(8,128)(2,1)S(1)} %copy-done), kind=kOutput, calls=%fused_computation.6 | convolution fusion | flops 4299161600 | bytes 12582912 | tf_op jit(solution)/shard_map/dot_general | solution.py:114
  73.6 0.0 reduce-scatter.3.cloned.1.call-update
  73.6 0.2 reduce-scatter.5.cloned.1.call-start
  73.9 136.7 %all-gather.2.cloned.1.call-done = bf16[2048,2048]{1,0:T(8,128)(2,1)} async-done(((bf16[256,2048]{1,0:T(8,128)(2,1)}), bf16[2048,2048]{1,0:T(8,128)(2,1)}) %all-gather.2.cloned.1.call-update) | async-done | bytes 8388624 | tf_op jit(solution)/shard_map/all_gather | solution.py:125
  210.5 9.0 %convolution_convert_fusion = bf16[512,2048]{1,0:T(8,128)(2,1)} fusion(bf16[512,2048]{1,0:T(8,128)(2,1)S(1)} %copy-done, bf16[2048,2048]{1,0:T(8,128)(2,1)} %all-gather.2.cloned.1.call-done), kind=kOutput, calls=%fused_computation.17 | convolution fusion | flops 4296015872 | bytes 12582912 | tf_op jit(solution)/shard_map/dot_general | solution.py:123
  219.6 4.1 %copy.47 = bf16[512,2048]{0,1:T(8,128)(2,1)} copy(bf16[512,2048]{1,0:T(8,128)(2,1)} %convolution_convert_fusion) | data formatting | bytes 4194304 | tf_op jit(solution)/shard_map/squeeze;reshape | solution.py:137
  223.6 11.1 %multiply_reduce_fusion = (f32[16,512]{1,0:T(8,128)S(1)}, f32[16,512,512]{1,2,0:T(8,128)}) fusion(f32[16,512,512]{1,2,0:T(8,128)} %get-tuple-element.13, f32[16,512]{1,0:T(8,128)S(1)} %get-tuple-element.12, bf16[512,16,128]{0,2,1:T(8,128)(2,1)} %bitcast.47, bf16[512,16,128]{0,2,1:T(8,128)(2,1)S(1)} %bitcast.45), kind=kOutput, calls=%fused_computation.2 | convolution fusion | flops 1086316544 | bytes 37814272 | tf_op jit(solution)/shard_map/qhd,khd->hqk/dot_general | solution.py:80
  234.7 0.0 reduce-scatter.5.cloned.1.call-update
  234.7 10.5 %fusion.9 = bf16[16,128,512]{2,1,0:T(8,128)(2,1)} fusion(bf16[512,16,128]{0,2,1:T(8,128)(2,1)} %bitcast.48, f32[16,512,512]{1,2,0:T(8,128)} %get-tuple-element.13, f32[16,512]{1,0:T(8,128)S(1)} %get-tuple-element.12), kind=kOutput, calls=%fused_computation.19 | convolution fusion | flops 1083179008 | bytes 21004288 | tf_op jit(solution)/shard_map/hqk,qhd->khd/dot_general | solution.py:77
  245.3 15.2 %multiply_convert_fusion = bf16[16,512,512]{1,2,0:T(8,128)(2,1)} fusion(f32[16,512,512]{1,2,0:T(8,128)} %get-tuple-element.15, f32[16,512]{1,0:T(8,128)S(1)} %get-tuple-element.14, f32[16,512,512]{1,2,0:T(8,128)} %get-tuple-element.13, f32[16,512]{1,0:T(8,128)S(1)} %get-tuple-element.12), kind=kLoop, calls=%fused_computation.1 | loop fusion | flops 16777216 | bytes 42008576 | tf_op jit(solution)/shard_map/convert_element_type | solution.py:84
  260.5 6.5 %reduce-scatter.5.cloned.1.call-done = bf16[256,2048]{0,1:T(8,128)(2,1)} async-done(((bf16[512,2048]{0,1:T(8,128)(2,1)}), bf16[256,2048]{0,1:T(8,128)(2,1)}) %reduce-scatter.5.cloned.1.call-update) | async-done | bytes 1048592 | tf_op jit(solution)/shard_map/reduce_scatter | solution.py:18
  267.0 2.3 copy.37
  269.3 7.5 %all-to-all-start.1 = ((bf16[16,16,2048]{2,1,0:T(8,128)(2,1)}), bf16[16,16,2048]{2,1,0:T(8,128)(2,1)S(1)}, u32[]{:S(2)}, u32[]{:S(2)}) async-start(bf16[16,16,2048]{2,1,0:T(8,128)(2,1)} %bitcast.41), calls=%async_computation.3 | async-start | bytes 2097152 | tf_op jit(solution)/shard_map/all_to_all | solution.py:29
  276.8 6.0 %multiply_convert_fusion.2 = bf16[16,512,128]{1,2,0:T(8,128)(2,1)} fusion(bf16[512,16,128]{0,2,1:T(8,128)(2,1)S(1)} %bitcast.38, bf16[16,512,512]{1,2,0:T(8,128)(2,1)} %multiply_convert_fusion), kind=kOutput, calls=%fused_computation.16 | convolution fusion | flops 1075838976 | bytes 12582912 | tf_op jit(solution)/shard_map/hqk,khd->qhd/dot_general | solution.py:87
  282.8 4.1 %copy.40 = bf16[512,2048]{1,0:T(8,128)(2,1)} copy(bf16[512,2048]{0,1:T(8,128)(2,1)} %bitcast.46) | data formatting | bytes 4194304
  286.9 2.4 copy.38
  289.2 8.3 %multiply_convert_fusion.1 = bf16[16,512,128]{1,2,0:T(8,128)(2,1)} fusion(bf16[16,512,512]{1,2,0:T(8,128)(2,1)} %multiply_convert_fusion, bf16[512,16,128]{0,2,1:T(8,128)(2,1)} %bitcast.43), kind=kOutput, calls=%fused_computation.15 | convolution fusion | flops 1075838976 | bytes 12582912 | tf_op jit(solution)/shard_map/hqk,qhd->khd/dot_general | solution.py:91
  297.5 3.9 %copy.39 = bf16[512,2048]{1,0:T(8,128)(2,1)} copy(bf16[512,2048]{0,1:T(8,128)(2,1)} %bitcast.49) | data formatting | bytes 4194304
  301.4 0.1 convert_reduce_fusion
  301.6 0.7 broadcast_multiply_fusion
  (13 shorter events, 0.0 us)
Async XLA Ops:
  8.0 58.8 %copy-start = (bf16[512,2048]{1,0:T(8,128)(2,1)S(1)}, bf16[512,2048]{1,0:T(8,128)(2,1)}, u32[]{:S(2)}) copy-start(bf16[512,2048]{1,0:T(8,128)(2,1)} %param.9) | copy-start | bytes 6291460
  8.0 202.5 %all-gather.2.cloned.1.call-start = ((), (), s32[]{:S(2)}) async-start(), calls=%async_computation.4 | async-start | bytes 9437184 | tf_op jit(solution)/shard_map/all_gather | solution.py:125
  35.0 199.7 %reduce-scatter.3.cloned.1.call-start = ((), (), s32[]{:S(2)}) async-start(), calls=%async_computation.5 | async-start | bytes 10485760 | tf_op jit(solution)/shard_map/reduce_scatter | solution.py:18
  39.0 7.9 %copy-start.5 = (s32[1,512]{1,0:T(1,128)S(1)}, s32[1,512]{1,0:T(1,128)}, u32[]{:S(2)}) copy-start(s32[1,512]{1,0:T(1,128)} %param.11) | copy-start | bytes 6148
  73.6 193.4 %reduce-scatter.5.cloned.1.call-start = ((), (), s32[]{:S(2)}) async-start(), calls=%async_computation.6 | async-start | bytes 3145728 | tf_op jit(solution)/shard_map/reduce_scatter | solution.py:18
  219.6 4.1 %copy-start.4 = (bf16[512,2048]{0,1:T(8,128)(2,1)S(1)}, bf16[512,2048]{0,1:T(8,128)(2,1)}, u32[]{:S(2)}) copy-start(bf16[512,2048]{0,1:T(8,128)(2,1)} %copy.48) | copy-start | bytes 6291460
  260.5 16.3 %copy-start.2 = (bf16[512,2048]{0,1:T(8,128)(2,1)S(1)}, bf16[512,2048]{0,1:T(8,128)(2,1)}, u32[]{:S(2)}) copy-start(bf16[512,2048]{0,1:T(8,128)(2,1)} %copy.45) | copy-start | bytes 6291460
  269.3 32.1 %all-to-all-start.1 = ((bf16[16,16,2048]{2,1,0:T(8,128)(2,1)}), bf16[16,16,2048]{2,1,0:T(8,128)(2,1)S(1)}, u32[]{:S(2)}, u32[]{:S(2)}) async-start(bf16[16,16,2048]{2,1,0:T(8,128)(2,1)} %bitcast.41), calls=%async_computation.3 | async-start | bytes 2097152 | tf_op jit(solution)/shard_map/all_to_all | solution.py:29
  282.8 4.1 %copy-start.3 = (bf16[16,512,128]{1,2,0:T(8,128)(2,1)S(1)}, bf16[16,512,128]{1,2,0:T(8,128)(2,1)}, u32[]{:S(2)}) copy-start(bf16[16,512,128]{1,2,0:T(8,128)(2,1)} %multiply_convert_fusion.2) | copy-start | bytes 6291460
  289.2 13.0 %copy-start.1 = (bf16[512,2048]{1,0:T(8,128)(2,1)S(1)}, bf16[512,2048]{1,0:T(8,128)(2,1)}, u32[]{:S(2)}) copy-start(bf16[512,2048]{1,0:T(8,128)(2,1)} %param.9) | copy-start | bytes 6291460
Sparse Core Ops, SparseCore 0:
  35.1 175.3 all-gather.1
Sparse Core Ops, SparseCore 1:
  73.7 136.1 reduce-scatter.2
  234.8 32.2 reduce-scatter.4
where the time goes:
time: 310 us
  waiting for transfers between devices  143 us (46%)
  matrix products  71.5 us (23%)
  local copies, waits for them, and re-layouts  29.6 us (10%)
  blocking collectives  25.8 us (8%)
  other arithmetic  16.2 us (5%)
  between operations  15.5 us (5%)
  starting transfers between devices  7.81 us (3%)
    all_gather x1, waiting for transfers between devices, shards(): lax.all_gather(group_rows, DP, axis=0, tiled=True)  137 us
    all_to_all x1, blocking collectives, sent_to_all(): lax.all_to_all(jnp.broadcast_to(value[None], (devices, *value.shape)), ax...  25.8 us
    convert_element_type x1, other arithmetic, attend_backward(): (probabilities * (grad_probs - row_inner)).astype(jnp.bfloat16)  15.2 us
    sub x1, matrix products, attend_forward(): raised = jnp.where(allowed, jnp.exp(masked - row_max), 0.0)  12 us
    dot_general x1, matrix products, attend_backward(): jnp.einsum('qhd,khd->hqk', grad_block, value_block, preferred_element_typ...  11.1 us
    dot_general x1, matrix products, attend_backward(): jnp.einsum('hqk,qhd->khd', probs_low, grad_block, preferred_element_type=...  10.5 us
    unnamed x15, local copies, waits for them, and re-layouts  10.4 us
    dot_general x1, matrix products, shards(): jnp.dot(columns, lax.all_gather(group_rows, DP, axis=0, tiled=True), pref...  9.02 us
  transfers between devices with their start and end apart: 4, of which 2 were waited for; matrix products, arithmetic and copies ran while one was open for 37% of the time, Pallas kernels for 0%

commit v1 on v0

v1 whole, which is shorter than its diff:
```python
import functools
import math

import jax
import jax.numpy as jnp
from jax import lax
from jax.experimental import pallas as pl
from jax.experimental.pallas import tpu as pltpu
from jax.sharding import PartitionSpec as P

H = 16
DH = 128
LEN = 512
HALF = 256
D = 2048
HD = 2048
RING = 4
ROWS = 16
SCALING = 1.0 / math.sqrt(DH)
SCALE2 = SCALING * math.log2(math.e)
NEG = -1e30
ALL = ("dp", "rep")
F32 = jnp.float32
BF16 = jnp.bfloat16
MESH = pl.DeviceIdType.MESH
EVERY = slice(None)

NN = (((1,), (0,)), ((), ()))
NT = (((1,), (1,)), ((), ()))
TN = (((0,), (0,)), ((), ()))

ORDERS = (("x", "y", "z"), ("y", "z", "x"), ("z", "x", "y"))
BOUNDS = (0, 640, 1280, 2048)
CUTS = (384, 1024, 1664)


def dot(a, b, dims=NN):
    return lax.dot_general(a, b, dims, preferred_element_type=F32)


def fill_bias(ids, bias_a, bias_b):
    start = jnp.zeros((1, LEN), jnp.int32)
    for v in range(3):
        count = jnp.sum((ids == v).astype(jnp.int32), axis=1, keepdims=True)
        start = start + jnp.where(ids > v, count, 0)
    t = lax.broadcasted_iota(jnp.int32, (HALF, LEN), 1)
    u = lax.broadcasted_iota(jnp.int32, (HALF, LEN), 0)
    bias_a[...] = jnp.where((u >= start) & (u <= t), 0.0, NEG).astype(F32)
    t = lax.broadcasted_iota(jnp.int32, (HALF, HALF), 1) + HALF
    u = lax.broadcasted_iota(jnp.int32, (HALF, HALF), 0) + HALF
    bias_b[...] = jnp.where((u >= start[:, HALF:]) & (u <= t), 0.0, NEG).astype(F32)


def head_forward(q, k, v, bias_a, bias_b):
    xa = dot(k[:HALF], q, NT) * SCALE2 + bias_a[...]
    xb = dot(k[HALF:], q[HALF:], NT) * SCALE2 + bias_b[...]
    ma = jnp.max(xa, axis=0, keepdims=True)
    mb = jnp.maximum(ma[:, HALF:], jnp.max(xb, axis=0, keepdims=True))
    m = jnp.concatenate([ma[:, :HALF], mb], axis=1)
    ea = jnp.exp2(xa - m)
    eb = jnp.exp2(xb - mb)
    la = jnp.sum(ea, axis=0, keepdims=True)
    lb = la[:, HALF:] + jnp.sum(eb, axis=0, keepdims=True)
    inv = 1.0 / jnp.concatenate([la[:, :HALF], lb], axis=1)
    pa = (ea * inv).astype(BF16)
    pb = (eb * inv[:, HALF:]).astype(BF16)
    vt = v.T
    ot_a = dot(vt[:, :HALF], pa)
    ot_b = dot(vt[:, HALF:], pb)
    ot = jnp.concatenate([ot_a[:, :HALF], ot_a[:, HALF:] + ot_b], axis=1)
    return ot.astype(BF16).T, pa, pb


def head_backward(q, k, v, g, low_a, low_b):
    q1, g1 = q[HALF:], g[HALF:]
    dpa = dot(v[:HALF], g, NT)
    dpb = dot(v[HALF:], g1, NT)
    pa = low_a.astype(F32)
    pb = low_b.astype(F32)
    ia = jnp.sum(pa * dpa, axis=0, keepdims=True)
    ib = ia[:, HALF:] + jnp.sum(pb * dpb, axis=0, keepdims=True)
    inner = jnp.concatenate([ia[:, :HALF], ib], axis=1)
    dsa = (pa * (dpa - inner)).astype(BF16)
    dsb = (pb * (dpb - ib)).astype(BF16)
    gv = (dot(low_a, g).astype(BF16), dot(low_b, g1).astype(BF16))
    gk = ((dot(dsa, q) * SCALING).astype(BF16), (dot(dsb, q1) * SCALING).astype(BF16))
    kt = k.T
    qt_a = dot(kt[:, :HALF], dsa)
    qt_b = dot(kt[:, HALF:], dsb)
    qt = jnp.concatenate([qt_a[:, :HALF], qt_a[:, HALF:] + qt_b], axis=1)
    return (qt * SCALING).astype(BF16).T, gk, gv


def kernel(
    ids, q_hbm, k_hbm, v_hbm, up_hbm, w_hbm, gq_hbm, gk_hbm, gv_hbm, gw_out,
    q, k, v, up, w, gw, pair, r1, r2p, r2m, ga, att, prob_a, prob_b, bias_a, bias_b,
    load_sem, out_sem, send_sem, recv_sem,
):
    dp, rep = lax.axis_index("dp"), lax.axis_index("rep")
    core = lax.rem(rep, 2)
    own = {
        "x": dp // 2,
        "y": lax.rem(rep // 2, RING),
        "z": (rep // 8) * 2 + lax.rem(dp, 2),
    }

    def near(dim, shift):
        at = dict(own)
        at[dim] = lax.rem(own[dim] + shift + RING, RING)
        x, y, z = at["x"], at["y"], at["z"]
        return (x * 2 + lax.rem(z, 2), (z // 2) * 8 + y * 2 + core)

    sibling = (dp, rep + 1 - 2 * core)

    def step(dim, shift):
        return lax.rem(own[dim] + shift + RING, RING)

    def place(at):
        x, y = at.get("x", EVERY), at.get("y", EVERY)
        if "z" in at:
            return (x, lax.rem(at["z"], 2), at["z"] // 2, y)
        return (x, EVERY, EVERY, y)

    def cols(lo, hi):
        return pl.ds(lo, hi - lo)

    started = []

    def send(src, dst, device):
        n = len(started)
        copy = pltpu.make_async_remote_copy(
            src_ref=src, dst_ref=dst, send_sem=send_sem.at[n], recv_sem=recv_sem.at[n],
            device_id=device, device_id_type=MESH,
        )
        copy.start()
        started.append(copy)
        return copy

    def arrived(copies):
        for copy in copies:
            copy.wait_recv()

    here = place(own)
    w_load = pltpu.make_async_copy(w_hbm, w.at[(*here, core)], load_sem.at[0])
    w_load.start()
    loads = []
    for c in range(3):
        part = cols(BOUNDS[c], BOUNDS[c + 1])
        group = []
        for i, (src, dst) in enumerate(((q_hbm, q), (k_hbm, k), (v_hbm, v))):
            copy = pltpu.make_async_copy(
                src.at[:, part], dst.at[:, part], load_sem.at[1 + 3 * c + i]
            )
            copy.start()
            group.append(copy)
        loads.append(group)
    up_load = pltpu.make_async_copy(up_hbm, up, load_sem.at[10])
    up_load.start()

    barrier = pltpu.get_barrier_semaphore()
    peers = [near(d, s) for d in ("x", "y", "z") for s in (1, -1, 2)] + [sibling]
    for peer in peers:
        pl.semaphore_signal(barrier, inc=1, device_id=peer, device_id_type=MESH)
    fill_bias(ids[...], bias_a, bias_b)
    pl.semaphore_wait(barrier, len(peers))
    w_load.wait()

    def share(at, lo, hi, device):
        ref = w.at[(*place(at), core, EVERY, cols(lo, hi))]
        return send(ref, ref, device)

    def spec(c):
        return (*ORDERS[c], BOUNDS[c], CUTS[c], BOUNDS[c + 1])

    crossed = []

    def cross(at, lo, hi):
        crossed.append(share(at, lo, hi, sibling))

    first = []
    for c in range(3):
        a, b, d, lo, mid, hi = spec(c)
        first += [share(own, lo, hi, near(a, s)) for s in (1, -1, 2)]

    def forward_pairs(lo, hi):
        def body(i, _):
            for j in range(2):
                h = i * 2 + j
                at = pl.ds(pl.multiple_of(h * DH, DH), DH)
                o, pa, pb = head_forward(q[:, at], k[:, at], v[:, at], bias_a, bias_b)
                att[:, at] = o
                prob_a[h] = pa
                prob_b[h] = pb
            return 0

        lax.fori_loop(lo, hi, body, 0)

    def weight_partial(c):
        lo, hi = BOUNDS[c], BOUNDS[c + 1]

        def body(i, _):
            rows = pl.ds(pl.multiple_of(i * 256, 256), 256)
            block = dot(up[:, rows], att[:, lo:hi], TN).astype(BF16)
            gw[i // 2, lax.rem(i, 2), :, :, :, :, cols(lo, hi)] = block.reshape(
                2, RING, 2, ROWS, hi - lo
            )
            return 0

        lax.fori_loop(0, 8, body, 0)
        part = cols(lo, hi)
        return send(
            gw.at[:, :, :, :, 1 - core, :, part], pair.at[:, :, :, :, :, part], sibling
        )

    def add_pair(c, copy):
        part = cols(BOUNDS[c], BOUNDS[c + 1])
        arrived([copy])

        def body(i, _):
            mine = gw[i, :, :, :, core, :, part].astype(F32)
            gw[i, :, :, :, core, :, part] = (
                mine + pair[i, :, :, :, :, part].astype(F32)
            ).astype(BF16)
            return 0

        lax.fori_loop(0, RING, body, 0)

    def gwi(at, lo, hi):
        return (*place(at), core, EVERY, cols(lo, hi))

    def bufi(at, lo, hi):
        return (*place(at), EVERY, cols(lo, hi))

    def ring_start(c, d, at, shifted):
        lo, mid, hi = BOUNDS[c], CUTS[c], BOUNDS[c + 1]
        far, up1, down1 = step(d, 2), step(d, 1), step(d, -1)
        far_at, up_at, down_at = ({**at, d: i} for i in (far, up1, down1))
        up_to, down_to = ({**shifted, d: i} for i in (up1, down1))
        return (
            [
                send(gw.at[gwi(far_at, lo, mid)], r1.at[bufi(far_at, lo, mid)], near(d, 1)),
                send(gw.at[gwi(far_at, mid, hi)], r1.at[bufi(far_at, mid, hi)], near(d, -1)),
            ],
            [
                send(gw.at[gwi(up_at, mid, hi)], r2p.at[bufi(up_to, mid, hi)], near(d, 1)),
                send(gw.at[gwi(down_at, lo, mid)], r2m.at[bufi(down_to, lo, mid)], near(d, -1)),
            ],
        )

    def ring_middle(c, d, at, shifted, state):
        lo, mid, hi = BOUNDS[c], CUTS[c], BOUNDS[c + 1]
        relayed, direct = state
        arrived(relayed)
        done = list(direct)
        for shift, l, h, buf in ((1, lo, mid, r2p), (-1, mid, hi, r2m)):
            spot = {**at, d: step(d, shift)}
            to = {**shifted, d: step(d, shift)}
            src = gwi(spot, l, h)
            gw[src] = (gw[src].astype(F32) + r1[bufi(spot, l, h)].astype(F32)).astype(BF16)
            done.append(send(gw.at[src], buf.at[bufi(to, l, h)], near(d, shift)))
        return done

    def ring_end(c, d, at, shifted, copies):
        lo, hi = BOUNDS[c], BOUNDS[c + 1]
        arrived(copies)
        spot = gwi({**at, d: own[d]}, lo, hi)
        got = bufi({**shifted, d: own[d]}, lo, hi)
        gw[spot] = (
            gw[spot].astype(F32) + r2p[got].astype(F32) + r2m[got].astype(F32)
        ).astype(BF16)

    def places(c, ring):
        a, b, d = ORDERS[c]
        if ring == 0:
            return (c, d, {}, {})
        return (c, b, {d: own[d]}, {d: step(d, 1)})

    def last_start(c):
        a, b, d, lo, mid, hi = spec(c)
        copies = []
        for shift, buf in ((1, r1), (-1, r2p), (2, r2m)):
            at = {**own, a: step(a, shift)}
            to = {**at, d: step(d, 2)}
            copies.append(send(gw.at[gwi(at, lo, hi)], buf.at[bufi(to, lo, hi)], near(a, shift)))
        return copies

    def last_end(c, copies):
        a, b, d, lo, mid, hi = spec(c)
        arrived(copies)
        got = bufi({**own, d: step(d, 2)}, lo, hi)
        total = gw[gwi(own, lo, hi)].astype(F32)
        for buf in (r1, r2p, r2m):
            total = total + buf[got].astype(F32)
        gw_out[:, lo:hi] = total * (1.0 / 256.0)

    state = {}

    def gather_first():
        arrived(first)
        out = []
        for c in range(3):
            a, b, d, lo, mid, hi = spec(c)
            at = {b: own[b], d: own[d]}
            out += [share(at, lo, hi, near(b, s)) for s in (1, -1)]
        state["ring"] = out
        state["sub"] = {}
        for c in range(3):
            sub_start(c, 0)
        for c in range(3):
            a, b, d, lo, mid, hi = spec(c)
            cross({b: own[b], d: own[d]}, lo, hi)

    def sub_start(c, shift):
        a, b, d, lo, mid, hi = spec(c)
        at = {b: step(b, shift), d: own[d]}
        state["sub"][c, shift] = [share(at, lo, hi, near(d, s)) for s in (1, -1)]

    def sub_middle(c, shift):
        a, b, d, lo, mid, hi = spec(c)
        arrived(state["sub"][c, shift])
        at = {b: step(b, shift)}
        below, above = {**at, d: step(d, -1)}, {**at, d: step(d, 1)}
        state["sub"][c, shift] = [
            share(below, lo, mid, near(d, 1)), share(above, mid, hi, near(d, -1))
        ]
        cross(below, lo, hi)
        cross(above, lo, hi)

    def sub_end(c, shift):
        a, b, d, lo, mid, hi = spec(c)
        arrived(state["sub"][c, shift])
        cross({b: step(b, shift), d: step(d, 2)}, lo, hi)

    def gather_second():
        arrived(state["ring"])
        out = []
        for c in range(3):
            a, b, d, lo, mid, hi = spec(c)
            below, above = {b: step(b, -1), d: own[d]}, {b: step(b, 1), d: own[d]}
            out += [share(below, lo, mid, near(b, 1)), share(above, mid, hi, near(b, -1))]
        state["ring"] = out
        for c in range(3):
            sub_start(c, 1)
            sub_start(c, -1)
        for c in range(3):
            a, b, d, lo, mid, hi = spec(c)
            cross({b: step(b, -1), d: own[d]}, lo, hi)
            cross({b: step(b, 1), d: own[d]}, lo, hi)

    def gather_third():
        arrived(state["ring"])
        for c in range(3):
            sub_start(c, 2)
        for c in range(3):
            a, b, d, lo, mid, hi = spec(c)
            cross({b: step(b, 2), d: own[d]}, lo, hi)

    def for_subs(f, shifts):
        for shift in shifts:
            for c in range(3):
                f(c, shift)

    arrived_load = lambda group: [copy.wait() for copy in group]
    arrived_load(loads[0])
    forward_pairs(0, 2)
    gather_first()
    arrived_load(loads[1])
    forward_pairs(2, 3)
    up_load.wait()
    gather_second()
    pair0 = weight_partial(0)
    gather_third()
    for_subs(sub_middle, (0,))
    forward_pairs(3, 5)
    add_pair(0, pair0)
    p0, q0 = places(0, 0), places(0, 1)
    ring0 = ring_start(*p0)
    pair1 = weight_partial(1)
    for_subs(sub_middle, (1, -1))
    for_subs(sub_end, (0,))
    arrived_load(loads[2])
    forward_pairs(5, 8)
    for_subs(sub_middle, (2,))
    add_pair(1, pair1)
    p1, q1 = places(1, 0), places(1, 1)
    ring1 = ring_start(*p1)
    for_subs(sub_end, (1, -1))
    pair2 = weight_partial(2)
    ring0 = ring_middle(*p0, ring0)
    for_subs(sub_end, (2,))
    add_pair(2, pair2)
    p2, q2 = places(2, 0), places(2, 1)
    ring2 = ring_start(*p2)
    arrived(crossed)

    def attended_grads(i, _):
        at = pl.ds(pl.multiple_of(i * 256, 256), 256)
        block = w[:, :, :, :, :, :, at].reshape(D, 256)
        ga[:, at] = dot(up[...], block).astype(BF16)
        return 0

    def backward_heads(lo, hi):
        def body(h, _):
            at = pl.ds(pl.multiple_of(h * DH, DH), DH)
            dq, dk, dv = head_backward(q[:, at], k[:, at], v[:, at], ga[:, at], prob_a[h], prob_b[h])
            q[:, at] = dq
            for i in range(2):
                k[i * HALF : (i + 1) * HALF, at] = dk[i]
                v[i * HALF : (i + 1) * HALF, at] = dv[i]
            return 0

        lax.fori_loop(lo, hi, body, 0)
        for i, (src, dst) in enumerate(((q, gq_hbm), (k, gk_hbm), (v, gv_hbm))):
            part = cols(lo * DH, hi * DH)
            copy = pltpu.make_async_copy(src.at[:, part], dst.at[:, part], out_sem.at[len(outs)])
            copy.start()
            outs.append(copy)

    outs = []
    lax.fori_loop(0, 4, attended_grads, 0)
    ring1 = ring_middle(*p1, ring1)
    ring_end(*p0, ring0)
    ring0 = ring_start(*q0)
    lax.fori_loop(4, 8, attended_grads, 0)
    ring2 = ring_middle(*p2, ring2)
    backward_heads(0, 3)
    ring0 = ring_middle(*q0, ring0)
    ring_end(*p1, ring1)
    ring1 = ring_start(*q1)
    backward_heads(3, 6)
    ring_end(*q0, ring0)
    last0 = last_start(0)
    ring1 = ring_middle(*q1, ring1)
    ring_end(*p2, ring2)
    ring2 = ring_start(*q2)
    backward_heads(6, 9)
    ring_end(*q1, ring1)
    last1 = last_start(1)
    ring2 = ring_middle(*q2, ring2)
    last_end(0, last0)
    backward_heads(9, 12)
    ring_end(*q2, ring2)
    last2 = last_start(2)
    last_end(1, last1)
    backward_heads(12, 16)
    last_end(2, last2)
    for copy in outs:
        copy.wait()
    for copy in started:
        copy.wait_send()


COPIES = 176


def whole(q, k, v, up, w, ids):
    chips = (RING, 2, 2, RING)
    wide = jax.ShapeDtypeStruct((LEN, HD), BF16)
    any_spec = pl.BlockSpec(memory_space=pl.ANY)
    vmem_spec = pl.BlockSpec(memory_space=pltpu.VMEM)
    return pl.pallas_call(
        kernel,
        in_specs=[vmem_spec] + [any_spec] * 5,
        out_specs=[any_spec] * 3 + [vmem_spec],
        out_shape=[wide] * 3 + [jax.ShapeDtypeStruct((ROWS, HD), F32)],
        scratch_shapes=[pltpu.VMEM((LEN, HD), BF16)] * 4
        + [pltpu.VMEM((*chips, 2, ROWS, HD), BF16)] * 2
        + [pltpu.VMEM((*chips, ROWS, HD), BF16)] * 4
        + [pltpu.VMEM((LEN, HD), BF16)] * 2
        + [pltpu.VMEM((H, HALF, LEN), BF16), pltpu.VMEM((H, HALF, HALF), BF16)]
        + [pltpu.VMEM((HALF, LEN), F32), pltpu.VMEM((HALF, HALF), F32)]
        + [
            pltpu.SemaphoreType.DMA((11,)),
            pltpu.SemaphoreType.DMA((15,)),
            pltpu.SemaphoreType.DMA((COPIES,)),
            pltpu.SemaphoreType.DMA((COPIES,)),
        ],
        compiler_params=pltpu.CompilerParams(
            collective_id=0, has_side_effects=True, vmem_limit_bytes=67_000_000
        ),
        name="whole",
    )(ids, q, k, v, up, w)


def shards(queries, key_rows, values, upstream, out_weight, sample_ids):
    return tuple(whole(queries, key_rows, values, upstream, out_weight, sample_ids))


def solution(mesh):
    return jax.shard_map(
        shards,
        mesh=mesh,
        in_specs=(P(ALL, None),) * 6,
        out_specs=(P(ALL, None),) * 4,
        check_vma=False,
    )
```

time: 310 us -> 84.8 us (0.27)
  waiting for transfers between devices: 143 us -> 0 us
  Pallas kernels: 0 us -> 75.6 us
  matrix products: 71.5 us -> 0 us
  blocking collectives: 25.8 us -> 0 us
  local copies, waits for them, and re-layouts: 29.6 us -> 7.64 us
  other arithmetic: 16.2 us -> 0 us
  between operations: 15.5 us -> 0.65 us
  starting transfers between devices: 7.81 us -> 0 us
    all_gather x1 -> x0, waiting for transfers between devices: 137 us -> none  [shards(): lax.all_gather(group_rows, DP, axis=0, tiled=True)]
    pallas_call x0 -> x1, Pallas kernels: none -> 75.6 us  [whole(): pl.pallas_call(kernel, in_specs=[vmem_spec] + [any_spec] * 5, out_specs=[...]
    dot_general x7 -> x0, matrix products: 59.5 us -> none  [the longest x1 11.1 us: attend_backward(): jnp.einsum('qhd,khd->hqk', grad_block, value_block, preferred_element_typ...]
    all_to_all x1 -> x0, blocking collectives: 25.8 us -> none  [sent_to_all(): lax.all_to_all(jnp.broadcast_to(value[None], (devices, *value.shape)), ax...]
    another operation x4 -> x0, local copies, waits for them, and re-layouts: 15.9 us -> none  [the longest x1 4.07 us: shards(): grad_attended[seq_index]]
    convert_element_type x1 -> x0, other arithmetic: 15.2 us -> none  [attend_backward(): (probabilities * (grad_probs - row_inner)).astype(jnp.bfloat16)]
    sub x1 -> x0, matrix products: 12 us -> none  [attend_forward(): raised = jnp.where(allowed, jnp.exp(masked - row_max), 0.0)]
    all_to_all x1 -> x0, starting transfers between devices: 7.5 us -> none  [sum_at_owner(): lax.all_to_all(cut_along(value, dim, devices), axis, 0, 0, tiled=True)]
  transfers between devices with their start and end apart: 4 -> 0, of which waited for: 2 -> 0; matrix products, arithmetic and copies ran while one was open for 37% -> 0% of each run, Pallas kernels for 0% -> 0%
where the time goes in v1:
time: 84.8 us; the launch traced here: 83.8 us
  Pallas kernels  75.6 us (89%)
  local copies, waits for them, and re-layouts  7.64 us (9%)
    pallas_call x1, Pallas kernels, whole(): pl.pallas_call(kernel, in_specs=[vmem_spec] + [any_spec] * 5, out_specs=[...  75.6 us
    unnamed x10, local copies, waits for them, and re-layouts  7.64 us

profile of v1, /device:TPU:1, one launch (start us, length us, event | category | flops | bytes accessed | tf_op | source)
XLA Modules:
  0.0 83.8 jit_solution(17451467294860493437)
XLA Ops:
  0.6 75.6 %whole.1 = (bf16[512,2048]{1,0:T(8,128)(2,1)}, bf16[512,2048]{1,0:T(8,128)(2,1)}, bf16[512,2048]{1,0:T(8,128)(2,1)}, f32[16,2048]{1,0:T(8,128)}) custom-call(s32[1,512]{1,0:T(1,128)} %ids.1, bf16[512,2048]{1,0:T(8,128)(2,1)} %q_hbm.1, bf16[512,2048]{1,0:T(8,128)(2,1)} %k_hbm.1, bf16[512,2048]{1,0:T(8,128)(2,1)} %v_hbm.1, bf16[512,2048]{1,0:T(8,128)(2,1)} %up_hbm.1, ...), custom_call_target="tpu_custom_call" | custom-call | tf_op jit(solution)/shard_map/whole/pallas_call | solution.py:461
  76.2 0.0 copy-start.1
  76.2 3.3 %copy.14 = bf16[512,2048]{1,0:T(8,128)(2,1)} copy(bf16[512,2048]{1,0:T(8,128)(2,1)} %get-tuple-element.8) | data formatting | bytes 4194304
  79.5 0.0 copy-done.1
  79.5 0.0 copy-start
  79.5 1.3 %copy.15 = bf16[512,2048]{1,0:T(8,128)(2,1)} copy(bf16[512,2048]{1,0:T(8,128)(2,1)S(1)} %copy-done.1) | data formatting | bytes 4194304
  80.8 1.0 %copy-done = bf16[512,2048]{1,0:T(8,128)(2,1)S(1)} copy-done((bf16[512,2048]{1,0:T(8,128)(2,1)S(1)}, bf16[512,2048]{1,0:T(8,128)(2,1)}, u32[]{:S(2)}) %copy-start) | copy-done | bytes 2097176
  81.9 0.0 copy-start.2
  81.9 1.3 %copy.16 = bf16[512,2048]{1,0:T(8,128)(2,1)} copy(bf16[512,2048]{1,0:T(8,128)(2,1)S(1)} %copy-done) | data formatting | bytes 4194304
  83.2 0.0 copy-done.2
  83.2 0.7 copy.17
Async XLA Ops:
  76.2 3.3 %copy-start.1 = (bf16[512,2048]{1,0:T(8,128)(2,1)S(1)}, bf16[512,2048]{1,0:T(8,128)(2,1)}, u32[]{:S(2)}) copy-start(bf16[512,2048]{1,0:T(8,128)(2,1)} %get-tuple-element.9) | copy-start | bytes 6291460
  79.5 2.3 %copy-start = (bf16[512,2048]{1,0:T(8,128)(2,1)S(1)}, bf16[512,2048]{1,0:T(8,128)(2,1)}, u32[]{:S(2)}) copy-start(bf16[512,2048]{1,0:T(8,128)(2,1)} %get-tuple-element.10) | copy-start | bytes 6291460
  81.9 1.3 %copy-start.2 = (f32[16,2048]{1,0:T(8,128)S(1)}, f32[16,2048]{1,0:T(8,128)}, u32[]{:S(2)}) copy-start(f32[16,2048]{1,0:T(8,128)} %get-tuple-element.11) | copy-start | bytes 393220

commit v2 on v1

v2 whole, which is shorter than its diff:
```python
import functools
import math

import jax
import jax.numpy as jnp
from jax import lax
from jax.experimental import pallas as pl
from jax.experimental.pallas import tpu as pltpu
from jax.sharding import PartitionSpec as P

H = 16
DH = 128
LEN = 512
HALF = 256
D = 2048
HD = 2048
RING = 4
ROWS = 16
SCALING = 1.0 / math.sqrt(DH)
SCALE2 = SCALING * math.log2(math.e)
NEG = -1e30
ALL = ("dp", "rep")
F32 = jnp.float32
BF16 = jnp.bfloat16
MESH = pl.DeviceIdType.MESH
EVERY = slice(None)

NN = (((1,), (0,)), ((), ()))
NT = (((1,), (1,)), ((), ()))
TN = (((0,), (0,)), ((), ()))

ORDERS = (("x", "y", "z"), ("y", "z", "x"), ("z", "x", "y"))
CHUNKS = ((0, 256, 512, 768), (768, 1024, 1280, 1536), (1536, 1664, 1792, 2048))


def dot(a, b, dims=NN):
    return lax.dot_general(a, b, dims, preferred_element_type=F32)


def fill_bias(ids, bias_a, bias_b):
    start = jnp.zeros((1, LEN), jnp.int32)
    for v in range(3):
        count = jnp.sum((ids == v).astype(jnp.int32), axis=1, keepdims=True)
        start = start + jnp.where(ids > v, count, 0)
    t = lax.broadcasted_iota(jnp.int32, (HALF, LEN), 1)
    u = lax.broadcasted_iota(jnp.int32, (HALF, LEN), 0)
    bias_a[...] = jnp.where((u >= start) & (u <= t), 0.0, NEG).astype(F32)
    t = lax.broadcasted_iota(jnp.int32, (HALF, HALF), 1) + HALF
    u = lax.broadcasted_iota(jnp.int32, (HALF, HALF), 0) + HALF
    bias_b[...] = jnp.where((u >= start[:, HALF:]) & (u <= t), 0.0, NEG).astype(F32)


def head_forward(q, k, v, bias_a, bias_b):
    xa = dot(k[:HALF], q, NT) * SCALE2 + bias_a[...]
    xb = dot(k[HALF:], q[HALF:], NT) * SCALE2 + bias_b[...]
    ma = jnp.max(xa, axis=0, keepdims=True)
    mb = jnp.maximum(ma[:, HALF:], jnp.max(xb, axis=0, keepdims=True))
    m = jnp.concatenate([ma[:, :HALF], mb], axis=1)
    ea = jnp.exp2(xa - m)
    eb = jnp.exp2(xb - mb)
    la = jnp.sum(ea, axis=0, keepdims=True)
    lb = la[:, HALF:] + jnp.sum(eb, axis=0, keepdims=True)
    inv = 1.0 / jnp.concatenate([la[:, :HALF], lb], axis=1)
    pa = (ea * inv).astype(BF16)
    pb = (eb * inv[:, HALF:]).astype(BF16)
    vt = v.T
    ot_a = dot(vt[:, :HALF], pa)
    ot_b = dot(vt[:, HALF:], pb)
    ot = jnp.concatenate([ot_a[:, :HALF], ot_a[:, HALF:] + ot_b], axis=1)
    return ot.astype(BF16).T, pa, pb


def head_backward(q, k, v, g, low_a, low_b):
    q1, g1 = q[HALF:], g[HALF:]
    dpa = dot(v[:HALF], g, NT)
    dpb = dot(v[HALF:], g1, NT)
    pa = low_a.astype(F32)
    pb = low_b.astype(F32)
    ia = jnp.sum(pa * dpa, axis=0, keepdims=True)
    ib = ia[:, HALF:] + jnp.sum(pb * dpb, axis=0, keepdims=True)
    inner = jnp.concatenate([ia[:, :HALF], ib], axis=1)
    dsa = (pa * (dpa - inner)).astype(BF16)
    dsb = (pb * (dpb - ib)).astype(BF16)
    gv = (dot(low_a, g).astype(BF16), dot(low_b, g1).astype(BF16))
    gk = ((dot(dsa, q) * SCALING).astype(BF16), (dot(dsb, q1) * SCALING).astype(BF16))
    kt = k.T
    qt_a = dot(kt[:, :HALF], dsa)
    qt_b = dot(kt[:, HALF:], dsb)
    qt = jnp.concatenate([qt_a[:, :HALF], qt_a[:, HALF:] + qt_b], axis=1)
    return (qt * SCALING).astype(BF16).T, gk, gv


def kernel(
    ids_hbm, q_hbm, k_hbm, v_hbm, up_hbm, w_hbm,
    q, k, v, gw_out,
    up, w, gw, pair, r1, r2p, r2m, att, prob_a, prob_b, bias_a, bias_b,
    ids, load_sem, send_sem, recv_sem, plane_sem,
):
    dp, rep = lax.axis_index("dp"), lax.axis_index("rep")
    core = lax.rem(rep, 2)
    own = {
        "x": dp // 2,
        "y": lax.rem(rep // 2, RING),
        "z": (rep // 8) * 2 + lax.rem(dp, 2),
    }

    def away(shifts):
        x, y, z = (lax.rem(own[d] + shifts.get(d, 0) + RING, RING) for d in ("x", "y", "z"))
        return (x * 2 + lax.rem(z, 2), (z // 2) * 8 + y * 2 + core)

    def near(dim, shift):
        return away({dim: shift})

    sibling = (dp, rep + 1 - 2 * core)

    def step(dim, shift):
        return lax.rem(own[dim] + shift + RING, RING)

    def place(at):
        x, y = (
            pl.ds(2 * i[0], 2) if isinstance(i, tuple) else i
            for i in (at.get("x", EVERY), at.get("y", EVERY))
        )
        z = at.get("z", EVERY)
        if isinstance(z, tuple):
            return (x, EVERY, z[0], y)
        if z is EVERY:
            return (x, EVERY, EVERY, y)
        return (x, lax.rem(z, 2), z // 2, y)

    def cols(lo, hi):
        return pl.ds(lo, hi - lo)

    groups = []

    def blob(k, part):
        lead = {
            3: (0, 0, 0, pl.ds(0, 3)),
            12: (pl.ds(0, 3), 0, 0, EVERY),
            16: (0, EVERY, EVERY, EVERY),
            32: (pl.ds(0, 2), EVERY, EVERY, EVERY),
            64: (EVERY, EVERY, EVERY, EVERY),
        }[k]
        return pair.at[(*lead, EVERY, part)]

    def group(k, n):
        groups.append(blob(k, chunk(n)))
        return len(groups) - 1

    def send(g, src, dst, device):
        pltpu.make_async_remote_copy(
            src_ref=src, dst_ref=dst, send_sem=send_sem.at[g], recv_sem=recv_sem.at[g],
            device_id=device, device_id_type=MESH,
        ).start()

    def arrived(g):
        pltpu.make_async_copy(groups[g], groups[g], recv_sem.at[g]).wait()

    def sent(g):
        pltpu.make_async_copy(groups[g], groups[g], send_sem.at[g]).wait()

    def chunk(n):
        return cols(CHUNKS[n][0], CHUNKS[n][3])

    def piece(n, c):
        return cols(CHUNKS[n][c], CHUNKS[n][c + 1])

    here = place(own)
    w_load = pltpu.make_async_copy(w_hbm, w.at[(*here, core)], load_sem.at[0])
    w_load.start()
    ids_load = pltpu.make_async_copy(ids_hbm, ids, load_sem.at[11])
    ids_load.start()
    loads = []
    for c in range(3):
        part = cols(CHUNKS[c][0], CHUNKS[c][3])
        trio = []
        for i, (src, dst) in enumerate(((q_hbm, q), (k_hbm, k), (v_hbm, v))):
            copy = pltpu.make_async_copy(
                src.at[:, part], dst.at[:, part], load_sem.at[1 + 3 * c + i]
            )
            copy.start()
            trio.append(copy)
        loads.append(trio)
    up_load = pltpu.make_async_copy(up_hbm, up, load_sem.at[10])
    up_load.start()

    barrier = pltpu.get_barrier_semaphore()
    beside = [near(d, s) for d in ("x", "y", "z") for s in (1, -1, 2)]
    peers = beside + [sibling]
    for peer in peers:
        pl.semaphore_signal(barrier, inc=1, device_id=peer, device_id_type=MESH)
    ids_load.wait()
    fill_bias(ids[...], bias_a, bias_b)
    pl.semaphore_wait(barrier, len(peers))
    w_load.wait()

    def share(g, at, part, device):
        ref = w.at[(*place(at), core, EVERY, part)]
        send(g, ref, ref, device)

    crossed = [group(64, n) for n in range(3)]
    row = [group(3, n) for n in range(3)]
    rest = [group(12, n) for n in range(3)]
    wide = [group(32, n) for n in range(3)]
    relay = [group(16, n) for n in range(3)]

    def cross(n, c, at):
        share(crossed[n], at, piece(n, c), sibling)

    def spread(n, shifts):
        for shift in shifts:
            for c in range(3):
                a, b, d = ORDERS[c]
                at = {b: step(b, shift), d: own[d]}
                for s in (1, -1):
                    share(wide[n], at, piece(n, c), near(d, s))

    def gather_a(n):
        arrived(row[n])
        spread(n, (0,))

    def gather_b(n):
        arrived(rest[n])
        spread(n, (1, -1, 2))
        for c in range(3):
            d = ORDERS[c][2]
            cross(n, c, {d: own[d]})

    def gather_d(n):
        arrived(wide[n])
        for c in range(3):
            a, b, d = ORDERS[c]
            for s, half in ((1, 0), (-1, 1)):
                share(relay[n], {b: (half,), d: step(d, -s)}, piece(n, c), near(d, s))
        for c in range(3):
            d = ORDERS[c][2]
            for s in (1, -1):
                cross(n, c, {d: step(d, s)})

    def gather_e(n):
        arrived(relay[n])
        for c in range(3):
            d = ORDERS[c][2]
            cross(n, c, {d: step(d, 2)})

    for n in range(3):
        for c in range(3):
            a, b, d = ORDERS[c]
            for s in (1, -1, 2):
                share(row[n], own, piece(n, c), near(a, s))
    for peer in beside:
        pl.semaphore_signal(plane_sem, inc=1, device_id=peer, device_id_type=MESH)

    def gather_rest():
        pl.semaphore_wait(plane_sem, len(beside))
        for n in range(3):
            for c in range(3):
                a, b, d = ORDERS[c]
                for sb in (1, -1, 2):
                    for sa in (0, 1, -1, 2):
                        share(rest[n], own, piece(n, c), away({a: sa, b: sb}))

    def forward_pairs(lo, hi):
        def body(i, _):
            for j in range(2):
                h = i * 2 + j
                at = pl.ds(pl.multiple_of(h * DH, DH), DH)
                o, pa, pb = head_forward(q[:, at], k[:, at], v[:, at], bias_a, bias_b)
                att[:, at] = o
                prob_a[h] = pa
                prob_b[h] = pb
            return 0

        lax.fori_loop(lo, hi, body, 0)

    def weight_partial(n, lo_i, hi_i):
        lo, hi = CHUNKS[n][0], CHUNKS[n][3]

        def body(i, _):
            rows = pl.ds(pl.multiple_of(i * 256, 256), 256)
            block = dot(up[:, rows], att[:, lo:hi], TN).astype(BF16)
            gw[i // 2, lax.rem(i, 2), :, :, :, :, cols(lo, hi)] = block.reshape(
                2, RING, 2, ROWS, hi - lo
            )
            return 0

        lax.fori_loop(lo_i, hi_i, body, 0)

    swaps, pairs = {}, {}

    def swap_pair(n, half):
        g = group(32, n)
        swaps[n, half] = g
        part, x = chunk(n), pl.ds(2 * half, 2)
        send(g, gw.at[x, :, :, :, 1 - core, :, part], pair.at[x, :, :, :, :, part], sibling)

    def add_pair(n):
        part = chunk(n)

        def body(i, _):
            mine = gw[i, :, :, :, core, :, part].astype(F32)
            gw[i, :, :, :, core, :, part] = (
                mine + pair[i, :, :, :, :, part].astype(F32)
            ).astype(BF16)
            return 0

        for half in range(2):
            arrived(swaps[n, half])
            lax.fori_loop(2 * half, 2 * half + 2, body, 0)

    def gwi(at, part):
        return (*place(at), core, EVERY, part)

    def bufi(at, part):
        return (*place(at), EVERY, part)

    rings = {}
    SIDES = ((1, 0, r2p), (-1, 1, r2m))

    def start(n):
        rings[n] = (group(16, n), group(32, n))
        for c in range(3):
            a, b, d = ORDERS[c]
            part = piece(n, c)
            for shift, half, buf in SIDES:
                far = {d: step(d, 2), b: (half,)}
                send(rings[n][0], gw.at[gwi(far, part)], r1.at[bufi(far, part)], near(d, shift))
        for c in range(3):
            a, b, d = ORDERS[c]
            part = piece(n, c)
            for shift, half, buf in SIDES:
                tail = {d: step(d, shift), b: (1 - half,)}
                send(rings[n][1], gw.at[gwi(tail, part)], buf.at[bufi(tail, part)], near(d, shift))

    def middle(n):
        arrived(rings[n][0])
        for c in range(3):
            a, b, d = ORDERS[c]
            part = piece(n, c)
            for shift, half, buf in SIDES:
                tail = {d: step(d, shift), b: (half,)}
                src = gwi(tail, part)
                gw[src] = (
                    gw[src].astype(F32) + r1[bufi(tail, part)].astype(F32)
                ).astype(BF16)
        for c in range(3):
            a, b, d = ORDERS[c]
            part = piece(n, c)
            for shift, half, buf in SIDES:
                tail = {d: step(d, shift), b: (half,)}
                send(rings[n][1], gw.at[gwi(tail, part)], buf.at[bufi(tail, part)], near(d, shift))

    def end(n):
        arrived(rings[n][1])
        for c in range(3):
            d = ORDERS[c][2]
            part = piece(n, c)
            spot, got = gwi({d: own[d]}, part), bufi({d: own[d]}, part)
            gw[spot] = (
                gw[spot].astype(F32) + r2p[got].astype(F32) + r2m[got].astype(F32)
            ).astype(BF16)

    OTHERS = [(sa, sb) for sb in (2, 1, -1, 0) for sa in (2, 1, -1, 0) if (sa, sb) != (0, 0)]

    def plane_start(n):
        rings[n] = (group(12, n), group(3, n))
        for i, (sa, sb) in enumerate(OTHERS):
            for c in range(3):
                a, b, d = ORDERS[c]
                part = piece(n, c)
                src = gw.at[gwi({**own, a: step(a, sa), b: step(b, sb)}, part)]
                dst = r1.at[bufi({**own, d: step(d, 2)}, part)]
                send(rings[n][i // 12], src, dst, away({a: sa, b: sb}))

    def plane_end(n):
        arrived(rings[n][0])
        arrived(rings[n][1])
        for c in range(3):
            a, b, d = ORDERS[c]
            part = piece(n, c)
            total = gw[gwi(own, part)].astype(F32)
            for sa, sb in OTHERS:
                at = {a: step(a, sa), b: step(b, sb), d: step(d, 2)}
                total = total + r1[bufi(at, part)].astype(F32)
            gw_out[:, part] = total * (1.0 / 256.0)

    def attended_grads_part(n):
        lax.fori_loop(CHUNKS[n][0] // 256, CHUNKS[n][3] // 256, attended_grads, 0)

    def attended_grads(i, _):
        at = pl.ds(pl.multiple_of(i * 256, 256), 256)
        block = w[:, :, :, :, :, :, at].reshape(D, 256)
        att[:, at] = dot(up[...], block).astype(BF16)
        return 0

    def backward_heads(lo, hi):
        def body(h, _):
            at = pl.ds(pl.multiple_of(h * DH, DH), DH)
            dq, dk, dv = head_backward(q[:, at], k[:, at], v[:, at], att[:, at], prob_a[h], prob_b[h])
            q[:, at] = dq
            for i in range(2):
                k[i * HALF : (i + 1) * HALF, at] = dk[i]
                v[i * HALF : (i + 1) * HALF, at] = dv[i]
            return 0

        lax.fori_loop(lo, hi, body, 0)

    def loaded(trio):
        for copy in trio:
            copy.wait()

    loaded(loads[0])
    forward_pairs(0, 2)
    gather_rest()
    forward_pairs(2, 3)
    up_load.wait()
    gather_a(0)
    gather_a(1)
    gather_a(2)
    weight_partial(0, 0, 4)
    swap_pair(0, 0)
    weight_partial(0, 4, 8)
    swap_pair(0, 1)
    loaded(loads[1])
    forward_pairs(3, 6)
    add_pair(0)
    gather_b(0)
    weight_partial(1, 0, 4)
    swap_pair(1, 0)
    gather_b(1)
    weight_partial(1, 4, 8)
    swap_pair(1, 1)
    gather_b(2)
    start(0)
    loaded(loads[2])
    forward_pairs(6, 7)
    gather_d(0)
    forward_pairs(7, 8)
    add_pair(1)
    start(1)
    weight_partial(2, 0, 4)
    swap_pair(2, 0)
    gather_d(1)
    weight_partial(2, 4, 8)
    swap_pair(2, 1)
    gather_d(2)
    gather_e(0)
    middle(0)
    arrived(crossed[0])
    attended_grads_part(0)
    add_pair(2)
    start(2)
    gather_e(1)
    middle(1)
    backward_heads(0, 2)
    end(0)
    gather_e(2)
    backward_heads(2, 4)
    middle(2)
    plane_start(0)
    backward_heads(4, 6)
    end(1)
    plane_start(1)
    arrived(crossed[1])
    attended_grads_part(1)
    end(2)
    plane_start(2)
    backward_heads(6, 9)
    plane_end(0)
    backward_heads(9, 12)
    arrived(crossed[2])
    attended_grads_part(2)
    backward_heads(12, 14)
    plane_end(1)
    backward_heads(14, 16)
    plane_end(2)
    for g in range(len(groups)):
        sent(g)


GROUPS = 36


def whole(q, k, v, up, w, ids):
    chips = (RING, 2, 2, RING)
    wide = jax.ShapeDtypeStruct((LEN, HD), BF16)
    hbm_spec = pl.BlockSpec(memory_space=pltpu.HBM)
    vmem_spec = pl.BlockSpec(memory_space=pltpu.VMEM)
    return pl.pallas_call(
        kernel,
        in_specs=[hbm_spec] * 6,
        out_specs=[vmem_spec] * 4,
        out_shape=[wide] * 3 + [jax.ShapeDtypeStruct((ROWS, HD), F32)],
        scratch_shapes=[pltpu.VMEM((LEN, HD), BF16)]
        + [pltpu.VMEM((*chips, 2, ROWS, HD), BF16)] * 2
        + [pltpu.VMEM((*chips, ROWS, HD), BF16)] * 4
        + [pltpu.VMEM((LEN, HD), BF16)]
        + [pltpu.VMEM((H, HALF, LEN), BF16), pltpu.VMEM((H, HALF, HALF), BF16)]
        + [pltpu.VMEM((HALF, LEN), F32), pltpu.VMEM((HALF, HALF), F32)]
        + [
            pltpu.VMEM((1, LEN), jnp.int32),
            pltpu.SemaphoreType.DMA((12,)),
            pltpu.SemaphoreType.DMA((GROUPS,)),
            pltpu.SemaphoreType.DMA((GROUPS,)),
            pltpu.SemaphoreType.REGULAR,
        ],
        compiler_params=pltpu.CompilerParams(
            collective_id=0, has_side_effects=True, vmem_limit_bytes=49_000_000
        ),
        name="whole",
    )(ids, q, k, v, up, w)


def pass_on_kernel(*refs):
    held, results, sems = refs[:4], refs[4:8], refs[8]
    copies = [
        pltpu.make_async_copy(src, dst, sems.at[i])
        for i, (src, dst) in enumerate(zip(held, results))
    ]
    for copy in copies:
        copy.start()
    for copy in copies:
        copy.wait()


def pass_on(*arrays):
    return pl.pallas_call(
        pass_on_kernel,
        in_specs=[pl.BlockSpec(memory_space=pltpu.VMEM)] * 4,
        out_specs=[pl.BlockSpec(memory_space=pltpu.HBM)] * 4,
        out_shape=[jax.ShapeDtypeStruct(a.shape, a.dtype) for a in arrays],
        scratch_shapes=[pltpu.SemaphoreType.DMA((4,))],
        compiler_params=pltpu.CompilerParams(vmem_limit_bytes=8_000_000),
        name="pass_on",
    )(*arrays)


def shards(queries, key_rows, values, upstream, out_weight, sample_ids):
    return tuple(pass_on(*whole(queries, key_rows, values, upstream, out_weight, sample_ids)))


def solution(mesh):
    return jax.shard_map(
        shards,
        mesh=mesh,
        in_specs=(P(ALL, None),) * 6,
        out_specs=(P(ALL, None),) * 4,
        check_vma=False,
    )
```

time: 84.8 us -> 62.1 us (0.73)
  Pallas kernels: 75.6 us -> 59.4 us
  local copies, waits for them, and re-layouts: 7.64 us -> 1.51 us
    pallas_call x1 -> x2, Pallas kernels: 75.6 us -> 59.4 us  [the longest x1 56.7 us: whole(): pl.pallas_call(kernel, in_specs=[hbm_spec] * 6, out_specs=[vmem_spec] * 4...]
    unnamed x10 -> x4, local copies, waits for them, and re-layouts: 7.64 us -> 1.51 us
where the time goes in v2:
time: 62.1 us; the launch traced here: 61.7 us
  Pallas kernels  59.4 us (96%)
  local copies, waits for them, and re-layouts  1.51 us (2%)
  between operations  0.81 us (1%)
    pallas_call x1, Pallas kernels, whole(): pl.pallas_call(kernel, in_specs=[hbm_spec] * 6, out_specs=[vmem_spec] * 4...  56.7 us
    pallas_call x1, Pallas kernels, pass_on(): pl.pallas_call(pass_on_kernel, in_specs=[pl.BlockSpec(memory_space=pltpu....  2.74 us
    unnamed x4, local copies, waits for them, and re-layouts  1.51 us

profile of v2, /device:TPU:1, one launch (start us, length us, event | category | flops | bytes accessed | tf_op | source)
XLA Modules:
  0.0 61.7 jit_solution(1229609373271043786)
XLA Ops:
  0.6 0.0 copy-start
  0.6 0.8 %copy-done = bf16[16,2048]{1,0:T(8,128)(2,1)S(1)} copy-done((bf16[16,2048]{1,0:T(8,128)(2,1)S(1)}, bf16[16,2048]{1,0:T(8,128)(2,1)}, u32[]{:S(2)}) %copy-start) | copy-done | bytes 65560
  1.5 0.0 copy-start.1
  1.5 0.7 %copy-done.1 = s32[1,512]{1,0:T(1,128)S(1)} copy-done((s32[1,512]{1,0:T(1,128)S(1)}, s32[1,512]{1,0:T(1,128)}, u32[]{:S(2)}) %copy-start.1) | copy-done | bytes 2072
  2.2 56.7 %whole.1 = (bf16[512,2048]{1,0:T(8,128)(2,1)S(1)}, bf16[512,2048]{1,0:T(8,128)(2,1)S(1)}, bf16[512,2048]{1,0:T(8,128)(2,1)S(1)}, f32[16,2048]{1,0:T(8,128)S(1)}) custom-call(s32[1,512]{1,0:T(1,128)S(1)} %copy-done.1, bf16[512,2048]{1,0:T(8,128)(2,1)} %q_hbm.1, bf16[512,2048]{1,0:T(8,128)(2,1)} %k_hbm.1, bf16[512,2048]{1,0:T(8,128)(2,1)} %v_hbm.1, ...), custom_call_target="tpu_custom_call" | custom-call | tf_op jit(solution)/shard_map/whole/pallas_call | solution.py:489
  58.8 2.7 %pass_on.1 = (bf16[512,2048]{1,0:T(8,128)(2,1)}, bf16[512,2048]{1,0:T(8,128)(2,1)}, bf16[512,2048]{1,0:T(8,128)(2,1)}, f32[16,2048]{1,0:T(8,128)}) custom-call(bf16[512,2048]{1,0:T(8,128)(2,1)S(1)} %get-tuple-element.8.refs_0_, bf16[512,2048]{1,0:T(8,128)(2,1)S(1)} %get-tuple-element.9.refs_1_, bf16[512,2048]{1,0:T(8,128)(2,1)S(1)} %get-tuple-element.10.refs_2_, ...), custom_call_target="tpu_custom_call" | custom-call | tf_op jit(solution)/shard_map/pass_on/pallas_call | solution.py:527
Async XLA Ops:
  0.6 0.8 %copy-start = (bf16[16,2048]{1,0:T(8,128)(2,1)S(1)}, bf16[16,2048]{1,0:T(8,128)(2,1)}, u32[]{:S(2)}) copy-start(bf16[16,2048]{1,0:T(8,128)(2,1)} %w_hbm.1) | copy-start | bytes 196612
  1.5 0.7 %copy-start.1 = (s32[1,512]{1,0:T(1,128)S(1)}, s32[1,512]{1,0:T(1,128)}, u32[]{:S(2)}) copy-start(s32[1,512]{1,0:T(1,128)} %ids_hbm.1) | copy-start | bytes 6148

commit v3 on v2

--- a/solution.py
+++ b/solution.py
@@ -93,7 +93,7 @@
 def kernel(
     ids_hbm, q_hbm, k_hbm, v_hbm, up_hbm, w_hbm,
     q, k, v, gw_out,
-    up, w, gw, pair, r1, r2p, r2m, att, prob_a, prob_b, bias_a, bias_b,
+    up, up_t, w, gw, pair, r1, r2p, r2m, att, prob_a, prob_b, bias_a, bias_b,
     ids, load_sem, send_sem, recv_sem, plane_sem,
 ):
     dp, rep = lax.axis_index("dp"), lax.axis_index("rep")
@@ -136,6 +136,8 @@
     def blob(k, part):
         lead = {
             3: (0, 0, 0, pl.ds(0, 3)),
+            4: (0, 0, 0, EVERY),
+            8: (0, 0, EVERY, EVERY),
             12: (pl.ds(0, 3), 0, 0, EVERY),
             16: (0, EVERY, EVERY, EVERY),
             32: (pl.ds(0, 2), EVERY, EVERY, EVERY),
@@ -165,6 +167,11 @@
     def piece(n, c):
         return cols(CHUNKS[n][c], CHUNKS[n][c + 1])
 
+    barrier = pltpu.get_barrier_semaphore()
+    beside = [near(d, s) for d in ("x", "y", "z") for s in (1, -1, 2)]
+    peers = beside + [sibling]
+    for peer in peers:
+        pl.semaphore_signal(barrier, inc=1, device_id=peer, device_id_type=MESH)
     here = place(own)
     w_load = pltpu.make_async_copy(w_hbm, w.at[(*here, core)], load_sem.at[0])
     w_load.start()
@@ -184,13 +191,6 @@
     up_load = pltpu.make_async_copy(up_hbm, up, load_sem.at[10])
     up_load.start()
 
-    barrier = pltpu.get_barrier_semaphore()
-    beside = [near(d, s) for d in ("x", "y", "z") for s in (1, -1, 2)]
-    peers = beside + [sibling]
-    for peer in peers:
-        pl.semaphore_signal(barrier, inc=1, device_id=peer, device_id_type=MESH)
-    ids_load.wait()
-    fill_bias(ids[...], bias_a, bias_b)
     pl.semaphore_wait(barrier, len(peers))
     w_load.wait()
 
@@ -199,13 +199,61 @@
         send(g, ref, ref, device)
 
     crossed = [group(64, n) for n in range(3)]
-    row = [group(3, n) for n in range(3)]
-    rest = [group(12, n) for n in range(3)]
-    wide = [group(32, n) for n in range(3)]
-    relay = [group(16, n) for n in range(3)]
+    gather = {}
 
     def cross(n, c, at):
         share(crossed[n], at, piece(n, c), sibling)
+
+    def gather_start(n):
+        gather[n] = group(3, n)
+        for c in range(3):
+            a, b, d = ORDERS[c]
+            for s in (1, -1, 2):
+                share(gather[n], own, piece(n, c), near(a, s))
+
+    def gather_a(n):
+        arrived(gather[n])
+        gather[n] = group(8, n)
+        for c in range(3):
+            a, b, d = ORDERS[c]
+            for s in (1, -1):
+                share(gather[n], {b: own[b], d: own[d]}, piece(n, c), near(b, s))
+
+    def gather_b(n):
+        arrived(gather[n])
+        gather[n] = group(4, n)
+        for c in range(3):
+            a, b, d = ORDERS[c]
+            for s, half in ((1, 0), (-1, 1)):
+                at = {a: (half,), b: step(b, -s), d: own[d]}
+                share(gather[n], at, piece(n, c), near(b, s))
+
+    def gather_c(n):
+        arrived(gather[n])
+        spread(n, (2,))
+        for c in range(3):
+            d = ORDERS[c][2]
+            cross(n, c, {d: own[d]})
+
+    def gather_d(n):
+        arrived(wide[n])
+        gather[n] = group(16, n)
+        for c in range(3):
+            a, b, d = ORDERS[c]
+            for s, half in ((1, 0), (-1, 1)):
+                share(gather[n], {b: (half,), d: step(d, -s)}, piece(n, c), near(d, s))
+        for c in range(3):
+            d = ORDERS[c][2]
+            for s in (1, -1):
+                cross(n, c, {d: step(d, s)})
+
+    def gather_e(n):
+        arrived(gather[n])
+        for c in range(3):
+            d = ORDERS[c][2]
+            cross(n, c, {d: step(d, 2)})
+
+    wide = [group(32, n) for n in range(3)]
 
     def spread(n, shifts):
         for shift in shifts:
@@ -215,57 +263,23 @@
                 for s in (1, -1):
                     share(wide[n], at, piece(n, c), near(d, s))
 
-    def gather_a(n):
-        arrived(row[n])
-        spread(n, (0,))
-
-    def gather_b(n):
-        arrived(rest[n])
-        spread(n, (1, -1, 2))
-        for c in range(3):
-            d = ORDERS[c][2]
-            cross(n, c, {d: own[d]})
-
-    def gather_d(n):
-        arrived(wide[n])
-        for c in range(3):
-            a, b, d = ORDERS[c]
-            for s, half in ((1, 0), (-1, 1)):
-                share(relay[n], {b: (half,), d: step(d, -s)}, piece(n, c), near(d, s))
-        for c in range(3):
-            d = ORDERS[c][2]
-            for s in (1, -1):
-                cross(n, c, {d: step(d, s)})
-
-    def gather_e(n):
-        arrived(relay[n])
-        for c in range(3):
-            d = ORDERS[c][2]
-            cross(n, c, {d: step(d, 2)})
-
     for n in range(3):
-        for c in range(3):
-            a, b, d = ORDERS[c]
-            for s in (1, -1, 2):
-                share(row[n], own, piece(n, c), near(a, s))
+        gather_start(n)
+
     for peer in beside:
         pl.semaphore_signal(plane_sem, inc=1, device_id=peer, device_id_type=MESH)
 
-    def gather_rest():
-        pl.semaphore_wait(plane_sem, len(beside))
-        for n in range(3):
-            for c in range(3):
-                a, b, d = ORDERS[c]
-                for sb in (1, -1, 2):
-                    for sa in (0, 1, -1, 2):
-                        share(rest[n], own, piece(n, c), away({a: sa, b: sb}))
+    ids_load.wait()
+    fill_bias(ids[...], bias_a, bias_b)
 
     def forward_pairs(lo, hi):
         def body(i, _):
+            done = []
             for j in range(2):
                 h = i * 2 + j
                 at = pl.ds(pl.multiple_of(h * DH, DH), DH)
-                o, pa, pb = head_forward(q[:, at], k[:, at], v[:, at], bias_a, bias_b)
+                done.append((h, at, head_forward(q[:, at], k[:, at], v[:, at], bias_a, bias_b)))
+            for h, at, (o, pa, pb) in done:
                 att[:, at] = o
                 prob_a[h] = pa
                 prob_b[h] = pb
@@ -277,16 +291,16 @@
         lo, hi = CHUNKS[n][0], CHUNKS[n][3]
 
         def body(i, _):
-            rows = pl.ds(pl.multiple_of(i * 256, 256), 256)
-            block = dot(up[:, rows], att[:, lo:hi], TN).astype(BF16)
-            gw[i // 2, lax.rem(i, 2), :, :, :, :, cols(lo, hi)] = block.reshape(
-                2, RING, 2, ROWS, hi - lo
-            )
+            rows = pl.ds(pl.multiple_of(i * 512, 512), 512)
+            if n == 0:
+                up_t[rows, :] = up[:, rows].T
+            block = dot(up_t[rows, :], att[:, lo:hi]).astype(BF16)
+            gw[i, :, :, :, :, :, cols(lo, hi)] = block.reshape(2, 2, RING, 2, ROWS, hi - lo)
             return 0
 
         lax.fori_loop(lo_i, hi_i, body, 0)
 
-    swaps, pairs = {}, {}
+    swaps = {}
 
     def swap_pair(n, half):
         g = group(32, n)
@@ -314,55 +328,84 @@
     def bufi(at, part):
         return (*place(at), EVERY, part)
 
+    def flow(n, c, ring):
+        a, b, d = ORDERS[c]
+        if ring == 0:
+            return (d, b, {}, {}, piece(n, c))
+        return (b, a, {d: own[d]}, {d: step(d, 1)}, piece(n, c))
+
     rings = {}
     SIDES = ((1, 0, r2p), (-1, 1, r2m))
 
-    def start(n):
-        rings[n] = (group(16, n), group(32, n))
-        for c in range(3):
-            a, b, d = ORDERS[c]
-            part = piece(n, c)
+    def start(n, ring):
+        relayed, direct = group(4 if ring else 16, n), group(8 if ring else 32, n)
+        rings[n] = (relayed, direct)
+        for c in range(3):
+            d, nxt, at, shifted, part = flow(n, c, ring)
             for shift, half, buf in SIDES:
-                far = {d: step(d, 2), b: (half,)}
-                send(rings[n][0], gw.at[gwi(far, part)], r1.at[bufi(far, part)], near(d, shift))
-        for c in range(3):
-            a, b, d = ORDERS[c]
-            part = piece(n, c)
+                far = {**at, d: step(d, 2), nxt: (half,)}
+                send(relayed, gw.at[gwi(far, part)], r1.at[bufi(far, part)], near(d, shift))
+        for c in range(3):
+            d, nxt, at, shifted, part = flow(n, c, ring)
             for shift, half, buf in SIDES:
-                tail = {d: step(d, shift), b: (1 - half,)}
-                send(rings[n][1], gw.at[gwi(tail, part)], buf.at[bufi(tail, part)], near(d, shift))
-
-    def middle(n):
-        arrived(rings[n][0])
-        for c in range(3):
-            a, b, d = ORDERS[c]
-            part = piece(n, c)
+                tail = {d: step(d, shift), nxt: (1 - half,)}
+                src = gw.at[gwi({**at, **tail}, part)]
+                send(direct, src, buf.at[bufi({**shifted, **tail}, part)], near(d, shift))
+
+    def middle(n, ring):
+        relayed, direct = rings[n]
+        arrived(relayed)
+        for c in range(3):
+            d, nxt, at, shifted, part = flow(n, c, ring)
             for shift, half, buf in SIDES:
-                tail = {d: step(d, shift), b: (half,)}
-                src = gwi(tail, part)
+                tail = {d: step(d, shift), nxt: (half,)}
+                src = gwi({**at, **tail}, part)
                 gw[src] = (
-                    gw[src].astype(F32) + r1[bufi(tail, part)].astype(F32)
+                    gw[src].astype(F32) + r1[bufi({**at, **tail}, part)].astype(F32)
                 ).astype(BF16)
         for c in range(3):
-            a, b, d = ORDERS[c]
-            part = piece(n, c)
+            d, nxt, at, shifted, part = flow(n, c, ring)
             for shift, half, buf in SIDES:
-                tail = {d: step(d, shift), b: (half,)}
-                send(rings[n][1], gw.at[gwi(tail, part)], buf.at[bufi(tail, part)], near(d, shift))
-
-    def end(n):
+                tail = {d: step(d, shift), nxt: (half,)}
+                src = gw.at[gwi({**at, **tail}, part)]
+                send(direct, src, buf.at[bufi({**shifted, **tail}, part)], near(d, shift))
+
+    def end(n, ring):
         arrived(rings[n][1])
         for c in range(3):
-            d = ORDERS[c][2]
-            part = piece(n, c)
-            spot, got = gwi({d: own[d]}, part), bufi({d: own[d]}, part)
+            d, nxt, at, shifted, part = flow(n, c, ring)
+            spot = gwi({**at, d: own[d]}, part)
+            got = bufi({**shifted, d: own[d]}, part)
             gw[spot] = (
                 gw[spot].astype(F32) + r2p[got].astype(F32) + r2m[got].astype(F32)
             ).astype(BF16)
 
+    def last_start(n):
+        rings[n] = group(3, n)
+        for c in range(3):
+            a, b, d = ORDERS[c]
+            for shift, buf in ((1, r1), (-1, r2p), (2, r2m)):
+                at = {**own, a: step(a, shift)}
+                to = {**at, d: step(d, 2)}
+                part = piece(n, c)
+                send(rings[n], gw.at[gwi(at, part)], buf.at[bufi(to, part)], near(a, shift))
+
+    def last_end(n):
+        arrived(rings[n])
+        for c in range(3):
+            d = ORDERS[c][2]
+            part = piece(n, c)
+            got = bufi({**own, d: step(d, 2)}, part)
+            total = gw[gwi(own, part)].astype(F32)
+            for buf in (r1, r2p, r2m):
+                total = total + buf[got].astype(F32)
+            gw_out[:, part] = total * (1.0 / 256.0)
+
     OTHERS = [(sa, sb) for sb in (2, 1, -1, 0) for sa in (2, 1, -1, 0) if (sa, sb) != (0, 0)]
 
     def plane_start(n):
+        if n == 1:
+            pl.semaphore_wait(plane_sem, len(beside))
         rings[n] = (group(12, n), group(3, n))
         for i, (sa, sb) in enumerate(OTHERS):
             for c in range(3):
@@ -394,91 +437,107 @@
         return 0
 
     def backward_heads(lo, hi):
-        def body(h, _):
-            at = pl.ds(pl.multiple_of(h * DH, DH), DH)
-            dq, dk, dv = head_backward(q[:, at], k[:, at], v[:, at], att[:, at], prob_a[h], prob_b[h])
-            q[:, at] = dq
-            for i in range(2):
-                k[i * HALF : (i + 1) * HALF, at] = dk[i]
-                v[i * HALF : (i + 1) * HALF, at] = dv[i]
+        def body(i, _):
+            done = []
+            for j in range(2):
+                h = i * 2 + j
+                at = pl.ds(pl.multiple_of(h * DH, DH), DH)
+                args = q[:, at], k[:, at], v[:, at], att[:, at], prob_a[h], prob_b[h]
+                done.append((at, head_backward(*args)))
+            for at, (dq, dk, dv) in done:
+                q[:, at] = dq
+                for i in range(2):
+                    k[i * HALF : (i + 1) * HALF, at] = dk[i]
+                    v[i * HALF : (i + 1) * HALF, at] = dv[i]
             return 0
 
-        lax.fori_loop(lo, hi, body, 0)
+        lax.fori_loop(lo // 2, hi // 2, body, 0)
 
     def loaded(trio):
         for copy in trio:
             copy.wait()
 
     loaded(loads[0])
-    forward_pairs(0, 2)
-    gather_rest()
-    forward_pairs(2, 3)
+    forward_pairs(0, 3)
     up_load.wait()
+    weight_partial(0, 0, 1)
     gather_a(0)
     gather_a(1)
     gather_a(2)
-    weight_partial(0, 0, 4)
+    spread(0, (0,))
+    spread(1, (0,))
+    spread(2, (0,))
+    weight_partial(0, 1, 2)
     swap_pair(0, 0)
-    weight_partial(0, 4, 8)
+    weight_partial(0, 2, 4)
     swap_pair(0, 1)
     loaded(loads[1])
-    forward_pairs(3, 6)
+    forward_pairs(3, 4)
+    gather_b(0)
+    spread(0, (1, -1))
+    gather_b(1)
+    spread(1, (1, -1))
+    forward_pairs(4, 5)
+    gather_b(2)
+    spread(2, (1, -1))
     add_pair(0)
-    gather_b(0)
-    weight_partial(1, 0, 4)
+    forward_pairs(5, 6)
+    gather_c(0)
+    gather_c(1)
+    weight_partial(1, 0, 2)
     swap_pair(1, 0)
-    gather_b(1)
-    weight_partial(1, 4, 8)
+    gather_c(2)
+    start(0, 0)
+    weight_partial(1, 2, 4)
     swap_pair(1, 1)
-    gather_b(2)
-    start(0)
+    gather_d(0)
     loaded(loads[2])
     forward_pairs(6, 7)
-    gather_d(0)
+    gather_d(1)
     forward_pairs(7, 8)
+    gather_d(2)
     add_pair(1)
-    start(1)
-    weight_partial(2, 0, 4)
+    middle(0, 0)
+    start(1, 0)
+    weight_partial(2, 0, 2)
     swap_pair(2, 0)
-    gather_d(1)
-    weight_partial(2, 4, 8)
+    weight_partial(2, 2, 4)
     swap_pair(2, 1)
-    gather_d(2)
     gather_e(0)
-    middle(0)
+    gather_e(1)
     arrived(crossed[0])
     attended_grads_part(0)
     add_pair(2)
-    start(2)
-    gather_e(1)
-    middle(1)
-    backward_heads(0, 2)
-    end(0)
+    start(2, 0)
     gather_e(2)
-    backward_heads(2, 4)
-    middle(2)
-    plane_start(0)
-    backward_heads(4, 6)
-    end(1)
-    plane_start(1)
+    end(0, 0)
+    start(0, 1)
+    backward_heads(0, 4)
+    middle(1, 0)
     arrived(crossed[1])
     attended_grads_part(1)
-    end(2)
+    middle(2, 0)
+    middle(0, 1)
+    backward_heads(4, 6)
+    end(1, 0)
+    plane_start(1)
+    backward_heads(6, 10)
+    end(2, 0)
     plane_start(2)
-    backward_heads(6, 9)
-    plane_end(0)
-    backward_heads(9, 12)
+    end(0, 1)
+    last_start(0)
+    backward_heads(10, 12)
     arrived(crossed[2])
     attended_grads_part(2)
-    backward_heads(12, 14)
     plane_end(1)
-    backward_heads(14, 16)
+    backward_heads(12, 16)
+    last_end(0)
     plane_end(2)
     for g in range(len(groups)):
         sent(g)
 
 
-GROUPS = 36
+GROUPS = 48
 
 
 def whole(q, k, v, up, w, ids):
@@ -491,7 +550,7 @@
         in_specs=[hbm_spec] * 6,
         out_specs=[vmem_spec] * 4,
         out_shape=[wide] * 3 + [jax.ShapeDtypeStruct((ROWS, HD), F32)],
-        scratch_shapes=[pltpu.VMEM((LEN, HD), BF16)]
+        scratch_shapes=[pltpu.VMEM((LEN, D), BF16), pltpu.VMEM((D, LEN), BF16)]
         + [pltpu.VMEM((*chips, 2, ROWS, HD), BF16)] * 2
         + [pltpu.VMEM((*chips, ROWS, HD), BF16)] * 4
         + [pltpu.VMEM((LEN, HD), BF16)]
@@ -505,7 +564,7 @@
             pltpu.SemaphoreType.REGULAR,
         ],
         compiler_params=pltpu.CompilerParams(
-            collective_id=0, has_side_effects=True, vmem_limit_bytes=49_000_000
+            collective_id=0, has_side_effects=True, vmem_limit_bytes=50_000_000
         ),
         name="whole",
     )(ids, q, k, v, up, w)

time: 62.1 us -> 57.7 us (0.929)
  Pallas kernels: 59.4 us -> 55.2 us
    pallas_call x1, Pallas kernels: 56.7 us -> 52.5 us  [whole(): pl.pallas_call(kernel, in_specs=[hbm_spec] * 6, out_specs=[vmem_spec] * 4...]
where the time goes in v3:
time: 57.7 us; the launch traced here: 57.5 us
  Pallas kernels  55.2 us (96%)
  local copies, waits for them, and re-layouts  1.51 us (3%)
  between operations  0.81 us (1%)
    pallas_call x1, Pallas kernels, whole(): pl.pallas_call(kernel, in_specs=[hbm_spec] * 6, out_specs=[vmem_spec] * 4...  52.5 us
    pallas_call x1, Pallas kernels, pass_on(): pl.pallas_call(pass_on_kernel, in_specs=[pl.BlockSpec(memory_space=pltpu....  2.74 us
    unnamed x4, local copies, waits for them, and re-layouts  1.51 us

profile of v3, /device:TPU:1, one launch (start us, length us, event | category | flops | bytes accessed | tf_op | source)
XLA Modules:
  0.0 57.5 jit_solution(5198470546267002241)
XLA Ops:
  0.6 0.0 copy-start
  0.6 0.8 %copy-done = bf16[16,2048]{1,0:T(8,128)(2,1)S(1)} copy-done((bf16[16,2048]{1,0:T(8,128)(2,1)S(1)}, bf16[16,2048]{1,0:T(8,128)(2,1)}, u32[]{:S(2)}) %copy-start) | copy-done | bytes 65560
  1.5 0.0 copy-start.1
  1.5 0.7 %copy-done.1 = s32[1,512]{1,0:T(1,128)S(1)} copy-done((s32[1,512]{1,0:T(1,128)S(1)}, s32[1,512]{1,0:T(1,128)}, u32[]{:S(2)}) %copy-start.1) | copy-done | bytes 2072
  2.2 52.5 %whole.1 = (bf16[512,2048]{1,0:T(8,128)(2,1)S(1)}, bf16[512,2048]{1,0:T(8,128)(2,1)S(1)}, bf16[512,2048]{1,0:T(8,128)(2,1)S(1)}, f32[16,2048]{1,0:T(8,128)S(1)}) custom-call(s32[1,512]{1,0:T(1,128)S(1)} %copy-done.1, bf16[512,2048]{1,0:T(8,128)(2,1)} %q_hbm.1, bf16[512,2048]{1,0:T(8,128)(2,1)} %k_hbm.1, bf16[512,2048]{1,0:T(8,128)(2,1)} %v_hbm.1, ...), custom_call_target="tpu_custom_call" | custom-call | tf_op jit(solution)/shard_map/whole/pallas_call | solution.py:548
  54.6 2.7 %pass_on.1 = (bf16[512,2048]{1,0:T(8,128)(2,1)}, bf16[512,2048]{1,0:T(8,128)(2,1)}, bf16[512,2048]{1,0:T(8,128)(2,1)}, f32[16,2048]{1,0:T(8,128)}) custom-call(bf16[512,2048]{1,0:T(8,128)(2,1)S(1)} %get-tuple-element.8.refs_0_, bf16[512,2048]{1,0:T(8,128)(2,1)S(1)} %get-tuple-element.9.refs_1_, bf16[512,2048]{1,0:T(8,128)(2,1)S(1)} %get-tuple-element.10.refs_2_, ...), custom_call_target="tpu_custom_call" | custom-call | tf_op jit(solution)/shard_map/pass_on/pallas_call | solution.py:586
Async XLA Ops:
  0.6 0.8 %copy-start = (bf16[16,2048]{1,0:T(8,128)(2,1)S(1)}, bf16[16,2048]{1,0:T(8,128)(2,1)}, u32[]{:S(2)}) copy-start(bf16[16,2048]{1,0:T(8,128)(2,1)} %w_hbm.1) | copy-start | bytes 196612
  1.5 0.7 %copy-start.1 = (s32[1,512]{1,0:T(1,128)S(1)}, s32[1,512]{1,0:T(1,128)}, u32[]{:S(2)}) copy-start(s32[1,512]{1,0:T(1,128)} %ids_hbm.1) | copy-start | bytes 6148

commit v4 on v3

--- a/solution.py
+++ b/solution.py
@@ -504,9 +504,9 @@
     weight_partial(2, 2, 4)
     swap_pair(2, 1)
     gather_e(0)
-    gather_e(1)
     arrived(crossed[0])
     attended_grads_part(0)
+    gather_e(1)
     add_pair(2)
     start(2, 0)
     gather_e(2)
@@ -519,9 +519,10 @@
     middle(2, 0)
     middle(0, 1)
     backward_heads(4, 6)
+    backward_heads(6, 8)
     end(1, 0)
     plane_start(1)
-    backward_heads(6, 10)
+    backward_heads(8, 10)
     end(2, 0)
     plane_start(2)
     end(0, 1)
@@ -529,8 +530,8 @@
     backward_heads(10, 12)
     arrived(crossed[2])
     attended_grads_part(2)
+    backward_heads(12, 16)
     plane_end(1)
-    backward_heads(12, 16)
     last_end(0)
     plane_end(2)
     for g in range(len(groups)):

time: 57.7 us -> 57.5 us (level)
  no operation moved by 1% of the time
where the time goes in v4:
time: 57.5 us; the launch traced here: 57.4 us
  Pallas kernels  55 us (96%)
  local copies, waits for them, and re-layouts  1.51 us (3%)
  between operations  0.81 us (1%)
    pallas_call x1, Pallas kernels, whole(): pl.pallas_call(kernel, in_specs=[hbm_spec] * 6, out_specs=[vmem_spec] * 4...  52.3 us
    pallas_call x1, Pallas kernels, pass_on(): pl.pallas_call(pass_on_kernel, in_specs=[pl.BlockSpec(memory_space=pltpu....  2.74 us
    unnamed x4, local copies, waits for them, and re-layouts  1.51 us

profile of v4, /device:TPU:1, one launch (start us, length us, event | category | flops | bytes accessed | tf_op | source)
XLA Modules:
  0.0 57.4 jit_solution(17183538267669938282)
XLA Ops:
  0.6 0.0 copy-start
  0.6 0.8 %copy-done = bf16[16,2048]{1,0:T(8,128)(2,1)S(1)} copy-done((bf16[16,2048]{1,0:T(8,128)(2,1)S(1)}, bf16[16,2048]{1,0:T(8,128)(2,1)}, u32[]{:S(2)}) %copy-start) | copy-done | bytes 65560
  1.5 0.0 copy-start.1
  1.5 0.7 %copy-done.1 = s32[1,512]{1,0:T(1,128)S(1)} copy-done((s32[1,512]{1,0:T(1,128)S(1)}, s32[1,512]{1,0:T(1,128)}, u32[]{:S(2)}) %copy-start.1) | copy-done | bytes 2072
  2.2 52.3 %whole.1 = (bf16[512,2048]{1,0:T(8,128)(2,1)S(1)}, bf16[512,2048]{1,0:T(8,128)(2,1)S(1)}, bf16[512,2048]{1,0:T(8,128)(2,1)S(1)}, f32[16,2048]{1,0:T(8,128)S(1)}) custom-call(s32[1,512]{1,0:T(1,128)S(1)} %copy-done.1, bf16[512,2048]{1,0:T(8,128)(2,1)} %q_hbm.1, bf16[512,2048]{1,0:T(8,128)(2,1)} %k_hbm.1, bf16[512,2048]{1,0:T(8,128)(2,1)} %v_hbm.1, ...), custom_call_target="tpu_custom_call" | custom-call | tf_op jit(solution)/shard_map/whole/pallas_call | solution.py:549
  54.5 2.7 %pass_on.1 = (bf16[512,2048]{1,0:T(8,128)(2,1)}, bf16[512,2048]{1,0:T(8,128)(2,1)}, bf16[512,2048]{1,0:T(8,128)(2,1)}, f32[16,2048]{1,0:T(8,128)}) custom-call(bf16[512,2048]{1,0:T(8,128)(2,1)S(1)} %get-tuple-element.8.refs_0_, bf16[512,2048]{1,0:T(8,128)(2,1)S(1)} %get-tuple-element.9.refs_1_, bf16[512,2048]{1,0:T(8,128)(2,1)S(1)} %get-tuple-element.10.refs_2_, ...), custom_call_target="tpu_custom_call" | custom-call | tf_op jit(solution)/shard_map/pass_on/pallas_call | solution.py:587
Async XLA Ops:
  0.6 0.8 %copy-start = (bf16[16,2048]{1,0:T(8,128)(2,1)S(1)}, bf16[16,2048]{1,0:T(8,128)(2,1)}, u32[]{:S(2)}) copy-start(bf16[16,2048]{1,0:T(8,128)(2,1)} %w_hbm.1) | copy-start | bytes 196612
  1.5 0.7 %copy-start.1 = (s32[1,512]{1,0:T(1,128)S(1)}, s32[1,512]{1,0:T(1,128)}, u32[]{:S(2)}) copy-start(s32[1,512]{1,0:T(1,128)} %ids_hbm.1) | copy-start | bytes 6148
